TPU v7x, 32 devices: a whole 2x2x4 slice. The times are simulated.
32 devices in a mesh: slab: 8 (over z, core), sub: 4 (over y, x).
Axes of the slice: x: 2, y: 2, z: 4, core: 2. Of those that a mesh axis runs over, the one named last changes fastest.
Arguments:
- child_moments: bfloat16 [216, 32768], P(None, ('slab', 'sub')), may hold values from -6 to 6
- incoming: bfloat16 [216, 4096], P(None, ('slab', 'sub')), may hold values from -6 to 6
- m2m_ops: bfloat16 [8, 216, 216], replicated, may hold values from -0.15625 to 0.15625
- m2l_ops: bfloat16 [160, 216, 216], P('sub'), may hold values from -0.046875 to 0.046875
- l2l_ops: bfloat16 [8, 216, 216], replicated, may hold values from -0.4375 to 0.4375
- partners: int32 [160, 4096], P(None, ('slab', 'sub')), may hold values from -1 to 4095, as said below
Outputs:
- child_locals: float32 [216, 32768], P(None, ('slab', 'sub'))
Inputs may be any that keep to these rules, and one draw needn't show every extreme that they name: `partners`: cells are numbered in Morton order of bricks of the domain, each brick one cell wide along the first dimension; the source of a pair lies in the same slab as its target or in an adjacent one, that is its id divided by 128 * 4 differs from the target's by at most one. Pairs are those of the interaction list: source and target are not adjacent, their parents are.
All inputs are finite; a program needn't handle non-finite values.
Results may differ from a plain program's by a relative error of at most 0.0035.
Values may be sent and summed in bfloat16 or wider, within the bound.
No kernel may reach another device: no remote copies, remote signals or barrier semaphores. Data moves between devices by JAX's collectives and lax.ppermute only.
A program may use at most 128 MiB of HBM per device.

v0:
```python
import jax
import jax.numpy as jnp
from jax import lax
from jax.sharding import PartitionSpec as P


def extended_2(block, sides, width):
    for axis, dim in sides:
        count = lax.axis_size(axis)
        forward = [(i, i + 1) for i in range(count - 1)]
        backward = [(target, source) for source, target in forward]
        low = lax.ppermute(
            lax.slice_in_dim(block, block.shape[dim] - width, None, axis=dim), axis, forward
        )
        high = lax.ppermute(lax.slice_in_dim(block, 0, width, axis=dim), axis, backward)
        block = jnp.concatenate([low, block, high], axis=dim)
    return block


def local(child_moments, incoming, m2m_ops, m2l_ops, l2l_ops, partners):
    order_cube = child_moments.shape[0]
    cell_count = child_moments.shape[1] // 8
    children = child_moments.reshape(order_cube, cell_count, 8)
    moments = jnp.einsum(
        "oij,jpo->ip", m2m_ops, children, preferred_element_type=jnp.float32
    ).astype(jnp.bfloat16)
    sub_count = lax.axis_size("sub")
    my_slab = lax.axis_index("slab")
    rim_cols = 32
    facing = jnp.concatenate([moments[:, :rim_cols], moments[:, cell_count - rim_cols :]], axis=1)
    padded = extended_2(facing, (("slab", 1),), rim_cols)
    below_top = padded[:, :rim_cols]
    above_bottom = padded[:, padded.shape[1] - rim_cols :]
    extended = jnp.concatenate([moments, below_top, above_bottom], axis=1)
    block_span = extended.shape[1]
    window = lax.all_gather(extended, "sub", axis=1, tiled=True)
    target_lists = lax.all_to_all(partners, "sub", split_axis=0, concat_axis=1, tiled=True)
    usable = target_lists >= 0
    slab_cells = cell_count * sub_count
    source_slab = target_lists // slab_cells
    within = target_lists % slab_cells
    source_sub = within // cell_count
    inner = within % cell_count
    delta = source_slab - my_slab
    column = jnp.where(
        delta == 0,
        inner,
        jnp.where(
            delta < 0, inner - (cell_count - rim_cols) + cell_count, inner + cell_count + rim_cols
        ),
    )
    offset_ids = jnp.where(usable, source_sub * block_span + column, 0)
    columns = jnp.take(window, offset_ids, axis=1)
    columns = jnp.where(usable[None, :, :], columns, jnp.zeros((), jnp.bfloat16))
    partial_terms = jnp.einsum("bij,jbc->ic", m2l_ops, columns, preferred_element_type=jnp.float32)
    far_field = lax.psum_scatter(partial_terms, "sub", scatter_dimension=1, tiled=True)
    locals_all = (incoming.astype(jnp.float32) + far_field).astype(jnp.bfloat16)
    child_out = jnp.einsum("oij,jp->ipo", l2l_ops, locals_all, preferred_element_type=jnp.float32)
    return child_out.reshape(order_cube, cell_count * 8)


def solution(mesh):
    in_specs = (
        P(None, ("slab", "sub")),
        P(None, ("slab", "sub")),
        P(),
        P("sub", None, None),
        P(),
        P(None, ("slab", "sub")),
    )
    out_specs = P(None, ("slab", "sub"))
    return jax.shard_map(local, mesh=mesh, in_specs=in_specs, out_specs=out_specs, check_vma=False)
```

profile of v0, /device:TPU:0, one launch (start us, length us, event | category | flops | bytes accessed | tf_op | source)
XLA Modules:
  0.0 168.5 jit_solution(7079776597476378982)
XLA Ops:
  6.5 0.0 copy-start
  6.5 1.3 copy.16
  7.8 1.6 fusion.11
  9.4 0.1 fusion.39
  9.5 2.4 %collective-permute-start = (bf16[216,32]{1,0:T(8,128)(2,1)S(1)}, bf16[216,32]{1,0:T(8,128)(2,1)S(1)}, u32[]{:S(2)}, u32[]{:S(2)}) collective-permute-start(bf16[216,32]{1,0:T(8,128)(2,1)S(1)} %get-tuple-element.7), channel_id=1, source_target_pairs={{0,4},{4,8},{8,12},{12,16},{16,20},{20,24},{24,28},{1,5},{5,9},{9,... | collective-permute-start | bytes 41480 | tf_op jit(solution)/shard_map/ppermute | solution.py:12
  11.9 1.3 collective-permute-start.1
  13.2 4.5 %all-to-all-start = ((s32[4,40,128]{2,1,0:T(8,128)}), s32[4,40,128]{2,1,0:T(8,128)S(1)}, u32[]{:S(2)}, u32[]{:S(2)}) async-start(s32[4,40,128]{2,1,0:T(8,128)} %bitcast.61), calls=%async_computation | async-start | bytes 163840 | tf_op jit(solution)/shard_map/all_to_all | solution.py:37
  17.8 0.0 reduce-scatter.2.cloned.1.call-start
  17.8 0.0 collective-permute-done
  17.8 0.0 collective-permute-done.1
  17.8 0.1 pad_maximum_fusion
  17.9 0.1 copy.18
  18.0 10.8 %all_gather.3 = bf16[216,768]{0,1:T(8,128)(2,1)S(1)} all-gather(bf16[216,192]{0,1:T(8,128)(2,1)S(1)} %copy.18), channel_id=1, replica_groups=mesh['slab'=8,'sub'=4] {'sub'}, dimensions={1}, use_global_device_ids=true | all-gather | bytes 414720 | tf_op jit(solution)/shard_map/all_gather | solution.py:36
  28.8 0.0 all-to-all-done
  28.9 0.2 fusion.21
  29.1 81.2 %gather_fusion = bf16[20480,216]{1,0:T(8,128)(2,1)} fusion(bf16[216,768]{0,1:T(8,128)(2,1)S(1)} %all_gather.3, s32[20480]{0:T(1024)S(1)} %broadcast_clamp_fusion), kind=kCustom, calls=%fused_computation | custom fusion | bytes 17776640 | tf_op jit(solution)/shard_map/jit(_take)/gather | solution.py:53
  110.4 13.1 %copy.20 = bf16[40,512,216]{1,2,0:T(8,128)(2,1)} copy(bf16[40,512,216]{2,1,0:T(8,128)(2,1)} %bitcast.56) | data formatting | bytes 17694720 | tf_op jit(solution)/shard_map/jit(_take)/gather | solution.py:53
  123.5 0.2 compare_and_fusion
  123.7 0.0 copy-start.1
  123.7 8.0 %fusion.8 = f32[216,512]{1,0:T(8,128)} fusion(bf16[40,216,216]{2,1,0:T(8,128)(2,1)} %param.9, bf16[40,512,216]{1,2,0:T(8,128)(2,1)} %copy.20, pred[40,512]{1,0:T(8,128)(4,1)S(1)} %get-tuple-element.6, pred[40,512]{1,0:T(8,128)(4,1)S(1)} %get-tuple-element.5), kind=kOutput, calls=%fused_computation.10 | convolution fusion | flops 1919877120 | bytes 13063168 | tf_op jit(solution)/shard_map/bij,jbc->ic/dot_general | solution.py:55
  131.8 0.0 reduce-scatter.2.cloned.1.call-update
  131.8 26.8 %reduce-scatter.2.cloned.1.call-done = f32[216,128]{1,0:T(8,128)} async-done(((f32[216,512]{1,0:T(8,128)}), f32[216,128]{1,0:T(8,128)}) %reduce-scatter.2.cloned.1.call-update) | async-done | bytes 110608 | tf_op jit(solution)/shard_map/reduce_scatter | solution.py:56
  158.6 0.0 copy-done
  158.6 0.0 copy-done.1
  158.6 1.3 convolution_bitcast_fusion
  159.9 0.5 copy.21
  160.4 1.2 copy.22
  (4 shorter events, 0.1 us)
Async XLA Ops:
  6.5 152.1 %copy-start = (bf16[8,216,216]{2,1,0:T(8,128)(2,1)S(1)}, bf16[8,216,216]{2,1,0:T(8,128)(2,1)}, u32[]{:S(2)}) copy-start(bf16[8,216,216]{2,1,0:T(8,128)(2,1)} %param.10) | copy-start | bytes 2239492
  9.5 8.3 %collective-permute-start = (bf16[216,32]{1,0:T(8,128)(2,1)S(1)}, bf16[216,32]{1,0:T(8,128)(2,1)S(1)}, u32[]{:S(2)}, u32[]{:S(2)}) collective-permute-start(bf16[216,32]{1,0:T(8,128)(2,1)S(1)} %get-tuple-element.7), channel_id=1, source_target_pairs={{0,4},{4,8},{8,12},{12,16},{16,20},{20,24},{24,28},{1,5},{5,9},{9,... | collective-permute-start | bytes 41480 | tf_op jit(solution)/shard_map/ppermute | solution.py:12
  11.9 5.9 %collective-permute-start.1 = (bf16[216,32]{1,0:T(8,128)(2,1)S(1)}, bf16[216,32]{1,0:T(8,128)(2,1)S(1)}, u32[]{:S(2)}, u32[]{:S(2)}) collective-permute-start(bf16[216,32]{1,0:T(8,128)(2,1)S(1)} %get-tuple-element.8), channel_id=1, source_target_pairs={{4,0},{8,4},{12,8},{16,12},{20,16},{24,20},{28,24},{5,1},{9,5},{13... | collective-permute-start | bytes 41480 | tf_op jit(solution)/shard_map/ppermute | solution.py:15
  13.2 15.6 %all-to-all-start = ((s32[4,40,128]{2,1,0:T(8,128)}), s32[4,40,128]{2,1,0:T(8,128)S(1)}, u32[]{:S(2)}, u32[]{:S(2)}) async-start(s32[4,40,128]{2,1,0:T(8,128)} %bitcast.61), calls=%async_computation | async-start | bytes 163840 | tf_op jit(solution)/shard_map/all_to_all | solution.py:37
  17.8 140.9 %reduce-scatter.2.cloned.1.call-start = ((), (), s32[]{:S(2)}) async-start(), calls=%async_computation.2 | async-start | bytes 552960 | tf_op jit(solution)/shard_map/reduce_scatter | solution.py:56
  123.7 34.9 %copy-start.1 = (bf16[216,128]{1,0:T(8,128)(2,1)S(1)}, bf16[216,128]{1,0:T(8,128)(2,1)}, u32[]{:S(2)}) copy-start(bf16[216,128]{1,0:T(8,128)(2,1)} %param.7) | copy-start | bytes 165892
Sparse Core Ops, SparseCore 0:
  131.9 26.6 reduce-scatter.1
where the time goes:
time: 169 us; the launch traced here: 168 us
  local copies, waits for them, and re-layouts  97.6 us (58%)
  waiting for transfers between devices  26.8 us (16%)
  between operations  13.5 us (8%)
  matrix products  10.9 us (6%)
  blocking collectives  10.8 us (6%)
  starting transfers between devices  8.24 us (5%)
    gather x2, local copies, waits for them, and re-layouts, local(): columns = jnp.take(window, offset_ids, axis=1)  94.4 us
    reduce_scatter x1, waiting for transfers between devices, local(): lax.psum_scatter(partial_terms, 'sub', scatter_dimension=1, tiled=True)  26.8 us
    all_gather x1, blocking collectives, local(): window = lax.all_gather(extended, 'sub', axis=1, tiled=True)  10.8 us
    dot_general x1, matrix products, local(): jnp.einsum('bij,jbc->ic', m2l_ops, columns, preferred_element_type=jnp.fl...  8.05 us
    all_to_all x1, starting transfers between devices, local(): lax.all_to_all(partners, 'sub', split_axis=0, concat_axis=1, tiled=True)  4.55 us
  transfers between devices with their start and end apart: 4, of which 1 were waited for; matrix products, arithmetic and copies ran while one was open for 0% of the time, Pallas kernels for 0%

commit v1 on v0

--- a/solution.py
+++ b/solution.py
@@ -33,7 +33,14 @@
     above_bottom = padded[:, padded.shape[1] - rim_cols :]
     extended = jnp.concatenate([moments, below_top, above_bottom], axis=1)
     block_span = extended.shape[1]
-    window = lax.all_gather(extended, "sub", axis=1, tiled=True)
+    peers = lax.axis_size("sub")
+    hops = [(i_2, (i_2 + 1) % peers) for i_2 in range(peers)]
+    parts = [extended]
+    for far in range(1, peers):
+        parts = [lax.ppermute(parts[0], "sub", hops), *parts]
+    full = jnp.concatenate(parts, axis=1)
+    places = (lax.axis_index("sub") + 1) * parts[-1].shape[1]
+    window = jnp.roll(full, places, axis=1)
     target_lists = lax.all_to_all(partners, "sub", split_axis=0, concat_axis=1, tiled=True)
     usable = target_lists >= 0
     slab_cells = cell_count * sub_count

time: 169 us -> 178 us (1.053)
  waiting for transfers between devices: 26.8 us -> 42.6 us
  blocking collectives: 10.8 us -> 0 us
  starting transfers between devices: 8.24 us -> 10.6 us
  local copies, waits for them, and re-layouts: 97.6 us -> 99.4 us
    ppermute x0 -> x3, waiting for transfers between devices: none -> 13.7 us  [local(): parts = [lax.ppermute(parts[0], 'sub', hops), *parts]]
    all_gather x1 -> x0, blocking collectives: 10.8 us -> none  [local(): window = lax.all_gather(extended, 'sub', axis=1, tiled=True)]
    all_to_all x1, waiting for transfers between devices: 0.01 us -> 2.71 us  [local(): lax.all_to_all(partners, 'sub', split_axis=0, concat_axis=1, tiled=True)]
    ppermute x0 -> x3, starting transfers between devices: none -> 2.37 us  [local(): parts = [lax.ppermute(parts[0], 'sub', hops), *parts]]
    concatenate x1, local copies, waits for them, and re-layouts: 0.1 us -> 1.89 us  [local(): window = jnp.roll(full, places, axis=1)]
  transfers between devices with their start and end apart: 4 -> 7, of which waited for: 1 -> 5; matrix products, arithmetic and copies ran while one was open for 0% -> 0% of each run, Pallas kernels for 0% -> 0%
where the time goes in v1:
time: 178 us; the launch traced here: 177 us
  local copies, waits for them, and re-layouts  99.4 us (56%)
  waiting for transfers between devices  42.6 us (24%)
  between operations  13.5 us (8%)
  matrix products  10.9 us (6%)
  starting transfers between devices  10.6 us (6%)
    gather x2, local copies, waits for them, and re-layouts, local(): columns = jnp.take(window, offset_ids, axis=1)  93.9 us
    reduce_scatter x1, waiting for transfers between devices, local(): lax.psum_scatter(partial_terms, 'sub', scatter_dimension=1, tiled=True)  26.1 us
    ppermute x3, waiting for transfers between devices, local(): parts = [lax.ppermute(parts[0], 'sub', hops), *parts]  13.7 us
    dot_general x1, matrix products, local(): jnp.einsum('bij,jbc->ic', m2l_ops, columns, preferred_element_type=jnp.fl...  8.05 us
    all_to_all x1, starting transfers between devices, local(): lax.all_to_all(partners, 'sub', split_axis=0, concat_axis=1, tiled=True)  4.55 us
  transfers between devices with their start and end apart: 7, of which 5 were waited for; matrix products, arithmetic and copies ran while one was open for 0% of the time, Pallas kernels for 0%

profile of v1, /device:TPU:0, one launch (start us, length us, event | category | flops | bytes accessed | tf_op | source)
XLA Modules:
  0.0 177.5 jit_solution(833746078150605111)
XLA Ops:
  6.5 0.0 copy-start
  6.5 1.3 copy.16
  7.8 1.6 fusion.11
  9.4 0.1 fusion.39
  9.5 2.4 %collective-permute-start = (bf16[216,32]{1,0:T(8,128)(2,1)S(1)}, bf16[216,32]{1,0:T(8,128)(2,1)S(1)}, u32[]{:S(2)}, u32[]{:S(2)}) collective-permute-start(bf16[216,32]{1,0:T(8,128)(2,1)S(1)} %get-tuple-element.7), channel_id=1, source_target_pairs={{0,4},{4,8},{8,12},{12,16},{16,20},{20,24},{24,28},{1,5},{5,9},{9,... | collective-permute-start | bytes 41480 | tf_op jit(solution)/shard_map/ppermute | solution.py:12
  11.9 1.3 collective-permute-start.1
  13.2 4.5 %all-to-all-start = ((s32[4,40,128]{2,1,0:T(8,128)}), s32[4,40,128]{2,1,0:T(8,128)S(1)}, u32[]{:S(2)}, u32[]{:S(2)}) async-start(s32[4,40,128]{2,1,0:T(8,128)} %bitcast.61), calls=%async_computation | async-start | bytes 163840 | tf_op jit(solution)/shard_map/all_to_all | solution.py:44
  17.8 0.0 reduce-scatter.2.cloned.1.call-start
  17.8 0.0 collective-permute-done
  17.8 0.0 collective-permute-done.1
  17.8 0.1 pad_maximum_fusion
  17.9 2.1 %collective-permute-start.2 = (bf16[216,192]{1,0:T(8,128)(2,1)S(1)}, bf16[216,192]{1,0:T(8,128)(2,1)S(1)}, u32[]{:S(2)}, u32[]{:S(2)}) collective-permute-start(bf16[216,192]{1,0:T(8,128)(2,1)S(1)} %pad_maximum_fusion), channel_id=1, source_target_pairs={{0,1},{1,2},{2,3},{3,0},{4,5},{5,6},{6,7},{7,4},{8,9},{9,10},{10,1... | collective-permute-start | bytes 248840 | tf_op jit(solution)/shard_map/ppermute | solution.py:40
  19.9 2.7 %all-to-all-done = s32[4,40,128]{2,1,0:T(8,128)S(1)} async-done(((s32[4,40,128]{2,1,0:T(8,128)}), s32[4,40,128]{2,1,0:T(8,128)S(1)}, u32[]{:S(2)}, u32[]{:S(2)}) %all-to-all-start) | async-done | bytes 81952 | tf_op jit(solution)/shard_map/all_to_all | solution.py:44
  22.7 0.2 fusion.21
  22.9 1.5 collective-permute-done.2
  24.5 0.3 collective-permute-start.3
  24.8 6.4 %collective-permute-done.3 = bf16[216,192]{1,0:T(8,128)(2,1)S(1)} collective-permute-done((bf16[216,192]{1,0:T(8,128)(2,1)S(1)}, bf16[216,192]{1,0:T(8,128)(2,1)S(1)}, u32[]{:S(2)}, u32[]{:S(2)}) %collective-permute-start.3) | collective-permute-done | bytes 82976 | tf_op jit(solution)/shard_map/ppermute | solution.py:40
  31.2 0.0 collective-permute-start.4
  31.2 0.2 compare_and_fusion
  31.4 5.8 %collective-permute-done.4 = bf16[216,192]{1,0:T(8,128)(2,1)S(1)} collective-permute-done((bf16[216,192]{1,0:T(8,128)(2,1)S(1)}, bf16[216,192]{1,0:T(8,128)(2,1)S(1)}, u32[]{:S(2)}, u32[]{:S(2)}) %collective-permute-start.4) | collective-permute-done | bytes 82976 | tf_op jit(solution)/shard_map/ppermute | solution.py:40
  37.2 1.9 %concatenate.11 = bf16[216,1536]{1,0:T(8,128)(2,1)S(1)} concatenate(bf16[216,192]{1,0:T(8,128)(2,1)S(1)} %collective-permute-done.4, bf16[216,192]{1,0:T(8,128)(2,1)S(1)} %collective-permute-done.3, bf16[216,192]{1,0:T(8,128)(2,1)S(1)} %collective-permute-done.2, bf16[216,128]{1,0:T(8,128)(2,1)S(1)} %fusion.11, bf16[216,32]{1,0:T(8,128)(2,1)S(1)} %collective-permute-done, ...), dimensions={1} | concatenate | bytes 1327104 | tf_op jit(solution)/shard_map/jit(_roll_dynamic)/concatenate | solution.py:43
  39.1 0.2 constant_dynamic-slice_fusion
  39.3 0.2 copy.19
  39.5 80.8 %gather_fusion = bf16[20480,216]{1,0:T(8,128)(2,1)} fusion(bf16[216,768]{0,1:T(8,128)(2,1)S(1)} %copy.19, s32[20480]{0:T(1024)S(1)} %broadcast_clamp_fusion), kind=kCustom, calls=%fused_computation | custom fusion | bytes 17776640 | tf_op jit(solution)/shard_map/jit(_take)/gather | solution.py:60
  120.2 13.2 %copy.20 = bf16[40,512,216]{1,2,0:T(8,128)(2,1)} copy(bf16[40,512,216]{2,1,0:T(8,128)(2,1)} %bitcast.56) | data formatting | bytes 17694720 | tf_op jit(solution)/shard_map/jit(_take)/gather | solution.py:60
  133.4 0.0 copy-start.1
  133.4 8.0 %fusion.8 = f32[216,512]{1,0:T(8,128)} fusion(bf16[40,216,216]{2,1,0:T(8,128)(2,1)} %param.9, bf16[40,512,216]{1,2,0:T(8,128)(2,1)} %copy.20, pred[40,512]{1,0:T(8,128)(4,1)S(1)} %get-tuple-element.6, pred[40,512]{1,0:T(8,128)(4,1)S(1)} %get-tuple-element.5), kind=kOutput, calls=%fused_computation.10 | convolution fusion | flops 1919877120 | bytes 13063168 | tf_op jit(solution)/shard_map/bij,jbc->ic/dot_general | solution.py:62
  141.4 0.0 reduce-scatter.2.cloned.1.call-update
  141.5 26.1 %reduce-scatter.2.cloned.1.call-done = f32[216,128]{1,0:T(8,128)} async-done(((f32[216,512]{1,0:T(8,128)}), f32[216,128]{1,0:T(8,128)}) %reduce-scatter.2.cloned.1.call-update) | async-done | bytes 110608 | tf_op jit(solution)/shard_map/reduce_scatter | solution.py:63
  167.6 0.0 copy-done
  167.6 0.0 copy-done.1
  167.6 1.3 convolution_bitcast_fusion
  168.9 0.5 copy.21
  169.4 1.2 copy.22
  (4 shorter events, 0.1 us)
Async XLA Ops:
  6.5 161.1 %copy-start = (bf16[8,216,216]{2,1,0:T(8,128)(2,1)S(1)}, bf16[8,216,216]{2,1,0:T(8,128)(2,1)}, u32[]{:S(2)}) copy-start(bf16[8,216,216]{2,1,0:T(8,128)(2,1)} %param.10) | copy-start | bytes 2239492
  9.5 8.3 %collective-permute-start = (bf16[216,32]{1,0:T(8,128)(2,1)S(1)}, bf16[216,32]{1,0:T(8,128)(2,1)S(1)}, u32[]{:S(2)}, u32[]{:S(2)}) collective-permute-start(bf16[216,32]{1,0:T(8,128)(2,1)S(1)} %get-tuple-element.7), channel_id=1, source_target_pairs={{0,4},{4,8},{8,12},{12,16},{16,20},{20,24},{24,28},{1,5},{5,9},{9,... | collective-permute-start | bytes 41480 | tf_op jit(solution)/shard_map/ppermute | solution.py:12
  11.9 5.9 %collective-permute-start.1 = (bf16[216,32]{1,0:T(8,128)(2,1)S(1)}, bf16[216,32]{1,0:T(8,128)(2,1)S(1)}, u32[]{:S(2)}, u32[]{:S(2)}) collective-permute-start(bf16[216,32]{1,0:T(8,128)(2,1)S(1)} %get-tuple-element.8), channel_id=1, source_target_pairs={{4,0},{8,4},{12,8},{16,12},{20,16},{24,20},{28,24},{5,1},{9,5},{13... | collective-permute-start | bytes 41480 | tf_op jit(solution)/shard_map/ppermute | solution.py:15
  13.2 9.4 %all-to-all-start = ((s32[4,40,128]{2,1,0:T(8,128)}), s32[4,40,128]{2,1,0:T(8,128)S(1)}, u32[]{:S(2)}, u32[]{:S(2)}) async-start(s32[4,40,128]{2,1,0:T(8,128)} %bitcast.61), calls=%async_computation | async-start | bytes 163840 | tf_op jit(solution)/shard_map/all_to_all | solution.py:44
  17.8 149.9 %reduce-scatter.2.cloned.1.call-start = ((), (), s32[]{:S(2)}) async-start(), calls=%async_computation.2 | async-start | bytes 552960 | tf_op jit(solution)/shard_map/reduce_scatter | solution.py:63
  17.9 6.6 %collective-permute-start.2 = (bf16[216,192]{1,0:T(8,128)(2,1)S(1)}, bf16[216,192]{1,0:T(8,128)(2,1)S(1)}, u32[]{:S(2)}, u32[]{:S(2)}) collective-permute-start(bf16[216,192]{1,0:T(8,128)(2,1)S(1)} %pad_maximum_fusion), channel_id=1, source_target_pairs={{0,1},{1,2},{2,3},{3,0},{4,5},{5,6},{6,7},{7,4},{8,9},{9,10},{10,1... | collective-permute-start | bytes 248840 | tf_op jit(solution)/shard_map/ppermute | solution.py:40
  24.5 6.7 %collective-permute-start.3 = (bf16[216,192]{1,0:T(8,128)(2,1)S(1)}, bf16[216,192]{1,0:T(8,128)(2,1)S(1)}, u32[]{:S(2)}, u32[]{:S(2)}) collective-permute-start(bf16[216,192]{1,0:T(8,128)(2,1)S(1)} %collective-permute-done.2), channel_id=1, source_target_pairs={{0,1},{1,2},{2,3},{3,0},{4,5},{5,6},{6,7},{7,4},{8,9},{9,10},{10,1... | collective-permute-start | bytes 248840 | tf_op jit(solution)/shard_map/ppermute | solution.py:40
  31.2 6.0 %collective-permute-start.4 = (bf16[216,192]{1,0:T(8,128)(2,1)S(1)}, bf16[216,192]{1,0:T(8,128)(2,1)S(1)}, u32[]{:S(2)}, u32[]{:S(2)}) collective-permute-start(bf16[216,192]{1,0:T(8,128)(2,1)S(1)} %collective-permute-done.3), channel_id=1, source_target_pairs={{0,1},{1,2},{2,3},{3,0},{4,5},{5,6},{6,7},{7,4},{8,9},{9,10},{10,1... | collective-permute-start | bytes 248840 | tf_op jit(solution)/shard_map/ppermute | solution.py:40
  133.4 34.2 %copy-start.1 = (bf16[216,128]{1,0:T(8,128)(2,1)S(1)}, bf16[216,128]{1,0:T(8,128)(2,1)}, u32[]{:S(2)}) copy-start(bf16[216,128]{1,0:T(8,128)(2,1)} %param.7) | copy-start | bytes 165892
Sparse Core Ops, SparseCore 0:
  141.6 25.9 reduce-scatter.1
